TPU v7x, 32 devices: a whole 2x2x4 slice. The times are simulated.
32 devices in a mesh: expert: 16 (over z, y, x), replica: 2 (over core).
Axes of the slice: x: 2, y: 2, z: 4, core: 2. Of those that a mesh axis runs over, the one named last changes fastest.
Arguments:
- a_tokens: bfloat16 [2048, 2048], P(('expert', 'replica')), may hold values from -6 to 6
- a_ids: int32 [2048, 6], P(('expert', 'replica')), may hold values from 0 to 15, all different within a row
- a_gates: float32 [2048, 6], P(('expert', 'replica')), may hold values from 0.05 to 0.6
- a_valid: int32 [2048], P(('expert', 'replica')), may hold values 0 or 1
- b_cot: bfloat16 [2048, 2048], P(('expert', 'replica')), may hold values from -0.86328125 to 0.86328125
- b_ids: int32 [2048, 6], P(('expert', 'replica')), may hold values from 0 to 15, all different within a row
- b_gates: float32 [2048, 6], P(('expert', 'replica')), may hold values from 0.05 to 0.6
- b_valid: int32 [2048], P(('expert', 'replica')), may hold values 0 or 1
- b_hidden: bfloat16 [16, 768, 704], P('expert', 'replica'), may hold values from -6 to 6
- w_gate: bfloat16 [16, 2048, 704], P('expert'), may hold values from -0.125 to 0.125
- w_up: bfloat16 [16, 2048, 704], P('expert'), may hold values from -0.125 to 0.125
- w_down: bfloat16 [16, 704, 2048], P('expert'), may hold values from -0.21875 to 0.21875
Outputs:
- a_out: bfloat16 [2048, 2048], P(('expert', 'replica'))
- grad_down: float32 [16, 704, 2048], P('expert', None, 'replica')
Inputs may be any that keep to these rules, and one draw needn't show every extreme that they name: `a_ids`: each token names 6 different experts. `b_ids`: each token names 6 different experts.
All inputs are finite; a program needn't handle non-finite values. No bound on the sum of `a_valid` or of `b_valid` on one device may be relied on, other than what follows from the above.
Results may differ from a plain program's by a relative error of at most 0.012.
Values may be sent and summed in bfloat16 or wider, within the bound.
No kernel may reach another device: no remote copies, remote signals or barrier semaphores. Data moves between devices by JAX's collectives and lax.ppermute only.
A program may use at most 64 MiB of HBM per device.

v0:
```python
import jax
import jax.numpy as jnp
from jax import lax
from jax.sharding import PartitionSpec as P


def slot_keys(expert_ids, valid_mask, experts, capacity):
    top_count = expert_ids.shape[1]
    flat_ids = expert_ids.reshape(-1)
    live = jnp.repeat(valid_mask, top_count) > 0
    onehot = (
        (flat_ids[:, None] == jnp.arange(experts, dtype=jnp.int32)[None, :]) & live[:, None]
    ).astype(jnp.int32)
    earlier = jnp.cumsum(onehot, axis=0) - onehot
    position = jnp.sum(earlier * onehot, axis=1)
    kept_mask = live & (position < capacity)
    return jnp.where(kept_mask, flat_ids * capacity + position, -1)


def gather_tokens(slot_key, tokens, experts, capacity):
    total = experts * capacity
    tok_count = tokens.shape[0]
    matches = jnp.arange(total, dtype=jnp.int32)[:, None] == slot_key[None, :]
    picker = jnp.any(matches.reshape(total, tok_count, -1), axis=2).astype(jnp.bfloat16)
    sent = jnp.dot(picker, tokens, preferred_element_type=jnp.float32).astype(jnp.bfloat16)
    return sent.reshape(experts, capacity, tokens.shape[1])


def gated_slots(slot_key, gate_values, cotangent, experts, capacity):
    total = experts * capacity
    tok_count = cotangent.shape[0]
    flat_gates = gate_values.reshape(-1)
    matches = jnp.arange(total, dtype=jnp.int32)[:, None] == slot_key[None, :]
    picker = jnp.any(matches.reshape(total, tok_count, -1), axis=2).astype(jnp.bfloat16)
    copied = jnp.dot(picker, cotangent, preferred_element_type=jnp.float32)
    slot_gate = jnp.sum(
        jnp.where(matches, flat_gates[None, :], jnp.zeros_like(flat_gates)[None, :]), axis=1
    )
    slots = copied * slot_gate[:, None]
    return slots.astype(jnp.bfloat16).reshape(experts, capacity, cotangent.shape[1])


def combine_slots(slot_key, gate_values, returned):
    model_width = returned.shape[-1]
    flat_rows = returned.reshape(-1, model_width)
    picked = flat_rows[jnp.maximum(slot_key, 0)]
    flat_gates = gate_values.reshape(-1)
    scale = jnp.where(slot_key >= 0, flat_gates, jnp.zeros_like(flat_gates))
    summed = picked.astype(flat_gates.dtype) * scale[:, None]
    return jnp.sum(
        summed.reshape(gate_values.shape[0], gate_values.shape[1], model_width), axis=1
    ).astype(jnp.bfloat16)


def expert_ffn(inputs, gate_weight, up_weight, down_weight):
    model_width = inputs.shape[-1]
    rows = inputs.reshape(-1, model_width)
    gate_proj = jnp.dot(rows, gate_weight, preferred_element_type=jnp.float32)
    up_proj = jnp.dot(rows, up_weight, preferred_element_type=jnp.float32)
    hidden = (jax.nn.silu(gate_proj) * up_proj).astype(jnp.bfloat16)
    result = jnp.dot(hidden, down_weight, preferred_element_type=jnp.float32).astype(jnp.bfloat16)
    return result.reshape(inputs.shape[:-1] + (down_weight.shape[1],))


def body(
    a_tokens,
    a_ids,
    a_gates,
    a_valid,
    b_cot,
    b_ids,
    b_gates,
    b_valid,
    b_hidden,
    w_gate,
    w_up,
    w_down,
):
    experts = lax.axis_size("expert")
    capacity = b_hidden.shape[1] // experts
    model_width = a_tokens.shape[1]
    a_keys = slot_keys(a_ids, a_valid, experts, capacity)
    a_send = gather_tokens(a_keys, a_tokens, experts, capacity)
    b_keys = slot_keys(b_ids, b_valid, experts, capacity)
    b_send = gated_slots(b_keys, b_gates, b_cot, experts, capacity)
    produced = expert_ffn(
        lax.all_to_all(a_send, "expert", split_axis=0, concat_axis=0, tiled=True),
        w_gate[0],
        w_up[0],
        w_down[0],
    )
    a_back = lax.all_to_all(produced, "expert", split_axis=0, concat_axis=0, tiled=True)
    b_recv = lax.all_to_all(b_send, "expert", split_axis=0, concat_axis=0, tiled=True)
    a_out = combine_slots(a_keys, a_gates, a_back)
    partial_grad = jnp.dot(
        b_hidden[0].T, b_recv.reshape(-1, model_width), preferred_element_type=jnp.float32
    )
    gradient = lax.psum_scatter(
        partial_grad.astype(jnp.bfloat16), "replica", scatter_dimension=1, tiled=True
    ).astype(jnp.float32)
    return (a_out, gradient[None])


def solution(mesh):
    placed = (
        P(("expert", "replica"), None),
        P(("expert", "replica"), None),
        P(("expert", "replica"), None),
        P(("expert", "replica")),
        P(("expert", "replica"), None),
        P(("expert", "replica"), None),
        P(("expert", "replica"), None),
        P(("expert", "replica")),
        P("expert", "replica", None),
        P("expert", None, None),
        P("expert", None, None),
        P("expert", None, None),
    )
    return jax.shard_map(
        body,
        mesh=mesh,
        in_specs=placed,
        out_specs=(P(("expert", "replica"), None), P("expert", None, "replica")),
        check_vma=False,
    )
```

profile of v0, /device:TPU:0, one launch (start us, length us, event | category | flops | bytes accessed | tf_op | source)
XLA Modules:
  0.0 177.7 jit_solution(7280205472322878811)
XLA Ops:
  7.2 0.0 copy-start
  7.2 0.8 broadcast_compare_fusion
  8.0 0.1 broadcast_in_dim.57
  8.1 0.2 gt.63
  8.2 0.1 gt.62
  8.4 0.8 copy.34
  9.2 0.1 eq.100
  9.3 0.1 eq.96
  9.4 0.9 reduce-window.16
  10.3 0.2 slice_reduce_fusion
  10.6 0.1 fusion.24
  10.7 0.1 reduce_sum.47
  10.8 0.7 broadcast_multiply_fusion.1
  11.5 0.8 copy.40
  12.3 0.1 broadcast_in_dim.59
  12.4 0.1 copy.38
  12.5 0.1 add_select_fusion
  12.6 0.1 copy.39
  12.7 0.2 fusion.19
  12.8 0.1 select_reduce_fusion
  13.0 2.7 %multiply_convert_fusion = bf16[384,2048]{1,0:T(8,128)(2,1)} fusion(pred[384,64]{0,1:T(8,128)(4,1)S(1)} %fusion.19, bf16[64,2048]{1,0:T(8,128)(2,1)} %param.16, f32[384]{0:T(512)S(1)} %select_reduce_fusion), kind=kOutput, calls=%fused_computation.3 | convolution fusion | flops 102236160 | bytes 1861120 | tf_op jit(solution)/shard_map/dot_general | solution.py:35
  15.7 0.0 copy-start.2
  15.7 0.0 copy-start.4
  15.7 0.0 copy-start.3
  15.7 0.0 copy-start.1
  15.7 8.5 %all-to-all-start.2 = ((bf16[16,24,2048]{2,1,0:T(8,128)(2,1)}), bf16[16,24,2048]{2,1,0:T(8,128)(2,1)}, u32[]{:S(2)}, u32[]{:S(2)}) async-start(bf16[16,24,2048]{2,1,0:T(8,128)(2,1)} %bitcast.78), calls=%async_computation.2 | async-start | bytes 3145728 | tf_op jit(solution)/shard_map/all_to_all | solution.py:93
  24.3 0.0 copy-done.2
  24.3 0.1 copy.28
  24.4 0.1 eq.89
  24.5 0.1 eq.85
  24.7 0.0 copy-done.4
  24.7 0.1 broadcast_in_dim.53
  24.7 0.2 gt.59
  24.9 0.1 gt.58
  25.1 0.9 reduce-window.14
  25.9 0.2 slice_reduce_fusion.1
  26.2 0.1 fusion.27
  26.3 0.1 reduce_sum.43
  26.4 0.0 copy-done.3
  26.4 0.1 copy.33
  26.5 0.1 compare_select_fusion
  26.6 0.1 copy.32
  26.7 0.2 fusion.18
  26.9 0.0 copy-done.1
  26.9 1.8 convolution_convert_fusion.1
  28.6 29.8 %all-to-all-done.2 = bf16[16,24,2048]{2,1,0:T(8,128)(2,1)} async-done(((bf16[16,24,2048]{2,1,0:T(8,128)(2,1)}), bf16[16,24,2048]{2,1,0:T(8,128)(2,1)}, u32[]{:S(2)}, u32[]{:S(2)}) %all-to-all-start.2) | async-done | bytes 1572896 | tf_op jit(solution)/shard_map/all_to_all | solution.py:93
  58.4 7.8 %all-to-all-start = ((bf16[16,24,2048]{2,1,0:T(8,128)(2,1)}), bf16[16,24,2048]{2,1,0:T(8,128)(2,1)}, u32[]{:S(2)}, u32[]{:S(2)}) async-start(bf16[16,24,2048]{2,1,0:T(8,128)(2,1)} %bitcast.79), calls=%async_computation | async-start | bytes 3145728 | tf_op jit(solution)/shard_map/all_to_all | solution.py:87
  66.2 0.0 reduce-scatter.2.cloned.1.call-start
  66.3 4.8 %fusion = bf16[704,2048]{1,0:T(8,128)(2,1)} fusion(bf16[384,2048]{1,0:T(8,128)(2,1)} %bitcast.10, bf16[1,384,704]{1,2,0:T(8,128)(2,1)} %param.20), kind=kOutput, calls=%fused_computation.4 | convolution fusion | flops 1108738048 | bytes 4997120 | tf_op jit(solution)/shard_map/dot_general | solution.py:95
  71.1 0.0 reduce-scatter.2.cloned.1.call-update
  71.1 28.7 %all-to-all-done = bf16[16,24,2048]{2,1,0:T(8,128)(2,1)} async-done(((bf16[16,24,2048]{2,1,0:T(8,128)(2,1)}), bf16[16,24,2048]{2,1,0:T(8,128)(2,1)}, u32[]{:S(2)}, u32[]{:S(2)}) %all-to-all-start) | async-done | bytes 1572896 | tf_op jit(solution)/shard_map/all_to_all | solution.py:87
  99.8 4.9 %fusion.5 = f32[384,704]{0,1:T(8,128)} fusion(bf16[384,2048]{1,0:T(8,128)(2,1)} %bitcast.2, bf16[1,2048,704]{1,2,0:T(8,128)(2,1)} %param.21), kind=kOutput, calls=%fused_computation.9 | convolution fusion | flops 1107296256 | bytes 5537792 | tf_op jit(solution)/shard_map/dot_general | solution.py:58
  104.7 0.0 copy-done
  104.7 6.7 %fusion.7 = bf16[384,2048]{1,0:T(8,128)(2,1)} fusion(bf16[1,704,2048]{2,1,0:T(8,128)(2,1)S(1)} %copy-done, bf16[384,2048]{1,0:T(8,128)(2,1)} %bitcast.2, bf16[1,2048,704]{1,2,0:T(8,128)(2,1)} %param.22, f32[384,704]{0,1:T(8,128)} %fusion.5), kind=kOutput, calls=%fused_computation.11 | convolution fusion | flops 2217000960 | bytes 9994240 | tf_op jit(solution)/shard_map/dot_general | solution.py:61
  111.5 7.3 %all-to-all-start.1 = ((bf16[16,24,2048]{2,1,0:T(8,128)(2,1)}), bf16[16,24,2048]{2,1,0:T(8,128)(2,1)}, u32[]{:S(2)}, u32[]{:S(2)}) async-start(bf16[16,24,2048]{2,1,0:T(8,128)(2,1)} %bitcast.80), calls=%async_computation.1 | async-start | bytes 3145728 | tf_op jit(solution)/shard_map/all_to_all | solution.py:92
  118.8 0.1 gt.60
  119.0 0.1 mul.64
  119.2 33.3 %all-to-all-done.1 = bf16[16,24,2048]{2,1,0:T(8,128)(2,1)} async-done(((bf16[16,24,2048]{2,1,0:T(8,128)(2,1)}), bf16[16,24,2048]{2,1,0:T(8,128)(2,1)}, u32[]{:S(2)}, u32[]{:S(2)}) %all-to-all-start.1) | async-done | bytes 1572896 | tf_op jit(solution)/shard_map/all_to_all | solution.py:92
  152.5 6.7 %gather_fusion = bf16[384,2048]{1,0:T(8,128)(2,1)} fusion(bf16[384,2048]{1,0:T(8,128)(2,1)} %bitcast.7, s32[1024]{0:T(1024)S(1)} %pad_clamp_fusion), kind=kCustom, calls=%fused_computation | custom fusion | bytes 3147264 | tf_op jit(solution)/shard_map/gather | solution.py:46
  159.1 3.9 %reshape.213 = f32[64,6,2048]{2,1,0:T(8,128)} reshape(bf16[384,2048]{1,0:T(8,128)(2,1)} %gather_fusion) | data formatting | bytes 4718592 | tf_op jit(solution)/shard_map/convert_element_type | solution.py:49
  163.0 4.5 %multiply_reduce_fusion = bf16[64,2048]{1,0:T(8,128)(2,1)} fusion(f32[64,6,2048]{2,1,0:T(8,128)} %reshape.213, f32[64,6]{1,0:T(8,128)S(1)} %get-tuple-element.2), kind=kLoop, calls=%fused_computation.1 | loop fusion | flops 1441792 | bytes 3409408 | tf_op jit(solution)/shard_map/reduce_sum | solution.py:50
  167.5 0.0 reduce-scatter.2.cloned.1.call-done
  167.5 3.3 %bitcast_convert_fusion = f32[1,704,1024]{2,1,0:T(8,128)} fusion(bf16[704,1024]{1,0:T(8,128)(2,1)} %reduce-scatter.2.cloned.1.call-done), kind=kLoop, calls=%fused_computation.13 | loop fusion | flops 720896 | bytes 4325376 | tf_op jit(solution)/shard_map/broadcast_in_dim | solution.py:101
  (9 shorter events, 0.1 us)
Async XLA Ops:
  7.2 97.6 %copy-start = (bf16[1,704,2048]{2,1,0:T(8,128)(2,1)S(1)}, bf16[1,704,2048]{2,1,0:T(8,128)(2,1)}, u32[]{:S(2)}) copy-start(bf16[1,704,2048]{2,1,0:T(8,128)(2,1)} %param.23) | copy-start | bytes 8650756
  15.7 8.6 %copy-start.2 = (s32[64,6]{0,1:T(8,128)S(1)}, s32[64,6]{0,1:T(8,128)}, u32[]{:S(2)}) copy-start(s32[64,6]{0,1:T(8,128)} %param.13) | copy-start | bytes 4612
  15.7 8.9 %copy-start.4 = (s32[64]{0:T(128)S(1)}, s32[64]{0:T(128)}, u32[]{:S(2)}) copy-start(s32[64]{0:T(128)} %param.15) | copy-start | bytes 772
  15.7 10.7 %copy-start.3 = (f32[64,6]{0,1:T(8,128)S(1)}, f32[64,6]{0,1:T(8,128)}, u32[]{:S(2)}) copy-start(f32[64,6]{0,1:T(8,128)} %param.14) | copy-start | bytes 4612
  15.7 11.1 %copy-start.1 = (bf16[64,2048]{1,0:T(8,128)(2,1)S(1)}, bf16[64,2048]{1,0:T(8,128)(2,1)}, u32[]{:S(2)}) copy-start(bf16[64,2048]{1,0:T(8,128)(2,1)} %param.12) | copy-start | bytes 786436
  15.7 42.7 %all-to-all-start.2 = ((bf16[16,24,2048]{2,1,0:T(8,128)(2,1)}), bf16[16,24,2048]{2,1,0:T(8,128)(2,1)}, u32[]{:S(2)}, u32[]{:S(2)}) async-start(bf16[16,24,2048]{2,1,0:T(8,128)(2,1)} %bitcast.78), calls=%async_computation.2 | async-start | bytes 3145728 | tf_op jit(solution)/shard_map/all_to_all | solution.py:93
  58.4 41.4 %all-to-all-start = ((bf16[16,24,2048]{2,1,0:T(8,128)(2,1)}), bf16[16,24,2048]{2,1,0:T(8,128)(2,1)}, u32[]{:S(2)}, u32[]{:S(2)}) async-start(bf16[16,24,2048]{2,1,0:T(8,128)(2,1)} %bitcast.79), calls=%async_computation | async-start | bytes 3145728 | tf_op jit(solution)/shard_map/all_to_all | solution.py:87
  66.2 101.3 %reduce-scatter.2.cloned.1.call-start = ((), (), s32[]{:S(2)}) async-start(), calls=%async_computation.4 | async-start | bytes 4325376 | tf_op jit(solution)/shard_map/reduce_scatter | solution.py:98
  111.5 41.0 %all-to-all-start.1 = ((bf16[16,24,2048]{2,1,0:T(8,128)(2,1)}), bf16[16,24,2048]{2,1,0:T(8,128)(2,1)}, u32[]{:S(2)}, u32[]{:S(2)}) async-start(bf16[16,24,2048]{2,1,0:T(8,128)(2,1)} %bitcast.80), calls=%async_computation.1 | async-start | bytes 3145728 | tf_op jit(solution)/shard_map/all_to_all | solution.py:92
Sparse Core Ops, SparseCore 0:
  71.2 11.8 reduce-scatter.1
where the time goes:
time: 180 us; the launch traced here: 178 us
  waiting for transfers between devices  91.8 us (51%)
  starting transfers between devices  23.7 us (13%)
  matrix products  21 us (12%)
  local copies, waits for them, and re-layouts  15 us (8%)
  between operations  14.2 us (8%)
  other arithmetic  12 us (7%)
    all_to_all x1, waiting for transfers between devices, body(): lax.all_to_all(produced, 'expert', split_axis=0, concat_axis=0, tiled=True)  33.3 us
    all_to_all x1, waiting for transfers between devices, body(): lax.all_to_all(b_send, 'expert', split_axis=0, concat_axis=0, tiled=True)  29.8 us
    all_to_all x1, waiting for transfers between devices, body(): lax.all_to_all(a_send, 'expert', split_axis=0, concat_axis=0, tiled=True)  28.7 us
    all_to_all x1, starting transfers between devices, body(): lax.all_to_all(b_send, 'expert', split_axis=0, concat_axis=0, tiled=True)  8.53 us
    all_to_all x1, starting transfers between devices, body(): lax.all_to_all(a_send, 'expert', split_axis=0, concat_axis=0, tiled=True)  7.79 us
    all_to_all x1, starting transfers between devices, body(): lax.all_to_all(produced, 'expert', split_axis=0, concat_axis=0, tiled=True)  7.33 us
    dot_general x1, matrix products, expert_ffn(): jnp.dot(hidden, down_weight, preferred_element_type=jnp.float32)  6.75 us
    gather x1, local copies, waits for them, and re-layouts, combine_slots(): picked = flat_rows[jnp.maximum(slot_key, 0)]  6.67 us
  transfers between devices with their start and end apart: 4, of which 3 were waited for; matrix products, arithmetic and copies ran while one was open for 20% of the time, Pallas kernels for 0%

commit v1 on v0

v1 whole, which is shorter than its diff:
```python
import jax
import jax.numpy as jnp
from jax import lax
from jax.sharding import PartitionSpec as P


def routing(ids, gates, valid, experts, capacity):
    eq = ids[:, :, None] == jnp.arange(experts, dtype=jnp.int32)[None, None, :]
    hit = jnp.any(eq, axis=1) & (valid > 0)[:, None]
    gate = jnp.sum(jnp.where(eq, gates[:, :, None], 0.0), axis=1)
    count = ids.shape[0]
    row = lax.broadcasted_iota(jnp.int32, (count, count), 0)
    col = lax.broadcasted_iota(jnp.int32, (count, count), 1)
    earlier = jnp.dot(
        (col < row).astype(jnp.bfloat16),
        hit.astype(jnp.bfloat16),
        preferred_element_type=jnp.float32,
    )
    slot = jnp.where(hit & (earlier < capacity), earlier, -1.0)
    return slot, gate


def pick_matrix(slot, capacity):
    at = jnp.arange(capacity, dtype=jnp.int32).astype(jnp.float32)
    return slot.T[:, None, :] == at[None, :, None]


def pick(slot, tokens, capacity):
    match = pick_matrix(slot, capacity)
    one = match.reshape(-1, tokens.shape[0]).astype(jnp.bfloat16)
    return jnp.dot(one, tokens, preferred_element_type=jnp.float32)


def pick_gated(slot, gate, cot, capacity):
    match = pick_matrix(slot, capacity)
    weight = jnp.sum(jnp.where(match, gate.T[:, None, :], 0.0), axis=2).reshape(-1)
    one = match.reshape(-1, cot.shape[0]).astype(jnp.bfloat16)
    copied = jnp.dot(one, cot, preferred_element_type=jnp.float32)
    return (copied * weight[:, None]).astype(jnp.bfloat16)


def combine(slot, gate, rows, capacity):
    at = jnp.arange(capacity, dtype=jnp.int32).astype(jnp.float32)
    coef = jnp.where(slot[:, :, None] == at[None, None, :], gate[:, :, None], 0.0)
    coef = coef.reshape(slot.shape[0], -1)
    high = lax.reduce_precision(coef, 8, 7)
    low = (coef - high).astype(jnp.bfloat16)
    high = high.astype(jnp.bfloat16)
    return jnp.dot(high, rows, preferred_element_type=jnp.float32) + jnp.dot(
        low, rows, preferred_element_type=jnp.float32
    )


def body(
    a_tokens,
    a_ids,
    a_gates,
    a_valid,
    b_cot,
    b_ids,
    b_gates,
    b_valid,
    b_hidden,
    w_gate,
    w_up,
    w_down,
):
    experts = lax.axis_size("expert")
    replicas = lax.axis_size("replica")
    half = experts // 2
    capacity = b_hidden.shape[1] // experts
    width = a_tokens.shape[1]
    count = a_tokens.shape[0]
    side = lax.axis_index("expert") // half
    across = [(e, (e + half) % experts) for e in range(experts)]
    groups = [[s * half + i for i in range(half)] for s in range(2)]

    def swap(x):
        return lax.ppermute(x, "expert", across)

    def spread(x):
        return lax.all_to_all(
            x, "expert", 0, 0, axis_index_groups=groups, tiled=True
        )

    a_far = swap(a_tokens)
    b_far = swap(b_cot)
    a_slot, a_gate = routing(a_ids, a_gates, a_valid, experts, capacity)
    b_slot, b_gate = routing(b_ids, b_gates, b_valid, experts, capacity)
    packed = jnp.stack([a_slot, a_gate, b_slot, b_gate])

    def take(x, which):
        return lax.dynamic_slice_in_dim(x, which * half, half, axis=x.ndim - 1)

    mine = take(packed, side)
    theirs = swap(take(packed, 1 - side))

    def both(x, y):
        x = x.reshape(half, 1, capacity, width)
        y = y.reshape(half, 1, capacity, width)
        return jnp.concatenate([x, y], axis=1).astype(jnp.bfloat16)

    a_send = both(
        pick(mine[0], a_tokens, capacity), pick(theirs[0], a_far, capacity)
    )
    rows = spread(a_send).reshape(-1, width)
    gate_proj = jnp.dot(rows, w_gate[0], preferred_element_type=jnp.float32)
    up_proj = jnp.dot(rows, w_up[0], preferred_element_type=jnp.float32)
    hidden = (jax.nn.silu(gate_proj) * up_proj).astype(jnp.bfloat16)
    made = jnp.dot(hidden, w_down[0], preferred_element_type=jnp.float32)
    made = made.astype(jnp.bfloat16).reshape(half, 2, capacity, width)
    back = spread(made)
    far_sum = combine(theirs[0], theirs[1], back[:, 1].reshape(-1, width), capacity)
    far_back = swap(far_sum.astype(jnp.bfloat16))
    near_sum = combine(mine[0], mine[1], back[:, 0].reshape(-1, width), capacity)
    a_out = (near_sum + far_back.astype(jnp.float32)).astype(jnp.bfloat16)

    b_send = both(
        pick_gated(mine[2], mine[3], b_cot, capacity),
        pick_gated(theirs[2], theirs[3], b_far, capacity),
    )
    b_rows = spread(b_send)
    held = b_hidden[0].reshape(2, half, capacity, -1)
    near_h = lax.dynamic_index_in_dim(held, side, 0, False)
    far_h = lax.dynamic_index_in_dim(held, 1 - side, 0, False)
    h_rows = jnp.stack([near_h, far_h], axis=1).reshape(-1, b_hidden.shape[2])
    b_rows = b_rows.reshape(-1, width)
    piece = width // replicas
    if replicas == 2:
        r = lax.axis_index("replica")

        def grad_of(which):
            cols = lax.dynamic_slice_in_dim(b_rows, which * piece, piece, axis=1)
            g = jnp.dot(h_rows.T, cols, preferred_element_type=jnp.float32)
            return g.astype(jnp.bfloat16)

        other = lax.ppermute(grad_of(1 - r), "replica", [(0, 1), (1, 0)])
        gradient = grad_of(r).astype(jnp.float32) + other.astype(jnp.float32)
    else:
        g = jnp.dot(h_rows.T, b_rows, preferred_element_type=jnp.float32)
        g = g.astype(jnp.bfloat16).reshape(-1, replicas, piece).swapaxes(0, 1)
        g = lax.all_to_all(g, "replica", 0, 0, tiled=True)
        gradient = jnp.sum(g.astype(jnp.float32), axis=0)
    return (a_out, gradient[None])


def solution(mesh):
    tokens = P(("expert", "replica"), None)
    flags = P(("expert", "replica"))
    held = P("expert", None, None)
    return jax.shard_map(
        body,
        mesh=mesh,
        in_specs=(tokens, tokens, tokens, flags) * 2
        + (P("expert", "replica", None), held, held, held),
        out_specs=(tokens, P("expert", None, "replica")),
        check_vma=False,
    )
```

time: 180 us -> 124 us (0.69)
  waiting for transfers between devices: 91.8 us -> 66.6 us
  between operations: 14.2 us -> 0.89 us
  local copies, waits for them, and re-layouts: 15 us -> 4.4 us
  other arithmetic: 12 us -> 6.26 us
  matrix products: 21 us -> 23.7 us
  starting transfers between devices: 23.7 us -> 21.3 us
    all_to_all x3, waiting for transfers between devices: 91.8 us -> 24.3 us  [spread(): lax.all_to_all(x, 'expert', 0, 0, axis_index_groups=groups, tiled=True)]
    ppermute x0 -> x5, waiting for transfers between devices: none -> 42.3 us  [the longest x4 42.3 us: swap(): return lax.ppermute(x, 'expert', across)]
    all_to_all x3, starting transfers between devices: 23.6 us -> 15.9 us  [spread(): lax.all_to_all(x, 'expert', 0, 0, axis_index_groups=groups, tiled=True)]
    gather x1 -> x0, local copies, waits for them, and re-layouts: 6.67 us -> none  [combine_slots(): picked = flat_rows[jnp.maximum(slot_key, 0)]]
    ppermute x0 -> x5, starting transfers between devices: none -> 5.43 us  [the longest x4 5.43 us: swap(): return lax.ppermute(x, 'expert', across)]
    convert_element_type x1 -> x0, local copies, waits for them, and re-layouts: 3.89 us -> none  [combine_slots(): summed = picked.astype(flat_gates.dtype) * scale[:, None]]
    broadcast_in_dim x1 -> x0, other arithmetic: 3.3 us -> none  [body(): return (a_out, gradient[None])]
    reduce_sum x4 -> x3, other arithmetic: 4.81 us -> 1.63 us  [the longest x2 1.44 us: routing(): gate = jnp.sum(jnp.where(eq, gates[:, :, None], 0.0), axis=1)]
  transfers between devices with their start and end apart: 4 -> 8, of which waited for: 3 -> 7; matrix products, arithmetic and copies ran while one was open for 20% -> 22% of each run, Pallas kernels for 0% -> 0%
where the time goes in v1:
time: 124 us; the launch traced here: 123 us
  waiting for transfers between devices  66.6 us (54%)
  matrix products  23.7 us (19%)
  starting transfers between devices  21.3 us (17%)
  other arithmetic  6.26 us (5%)
  local copies, waits for them, and re-layouts  4.4 us (4%)
    ppermute x4, waiting for transfers between devices, swap(): return lax.ppermute(x, 'expert', across)  42.3 us
    all_to_all x3, waiting for transfers between devices, spread(): lax.all_to_all(x, 'expert', 0, 0, axis_index_groups=groups, tiled=True)  24.3 us
    all_to_all x3, starting transfers between devices, spread(): lax.all_to_all(x, 'expert', 0, 0, axis_index_groups=groups, tiled=True)  15.9 us
    dot_general x2, matrix products, grad_of(): g = jnp.dot(h_rows.T, cols, preferred_element_type=jnp.float32)  7.37 us
    dot_general x1, matrix products, body(): made = jnp.dot(hidden, w_down[0], preferred_element_type=jnp.float32)  6.74 us
    ppermute x4, starting transfers between devices, swap(): return lax.ppermute(x, 'expert', across)  5.43 us
    dot_general x1, matrix products, body(): gate_proj = jnp.dot(rows, w_gate[0], preferred_element_type=jnp.float32)  4.98 us
  transfers between devices with their start and end apart: 8, of which 7 were waited for; matrix products, arithmetic and copies ran while one was open for 22% of the time, Pallas kernels for 0%

profile of v1, /device:TPU:0, one launch (start us, length us, event | category | flops | bytes accessed | tf_op | source)
XLA Modules:
  0.0 123.1 jit_solution(5470122798190980623)
XLA Ops:
  0.6 0.0 copy-start
  0.7 0.9 fusion.34
  1.5 0.7 fusion.33
  2.2 0.7 select_reduce_fusion.3
  2.9 0.7 select_reduce_fusion.2
  3.7 0.7 broadcast_compare_fusion
  4.4 0.1 select_bitcast_fusion
  4.5 0.1 select_bitcast_fusion.1
  4.7 4.1 %collective-permute-start = (f32[4,64,8]{1,2,0:T(8,128)S(1)}, f32[4,64,8]{1,2,0:T(8,128)S(1)}, u32[]{:S(2)}, u32[]{:S(2)}) collective-permute-start(f32[4,64,8]{1,2,0:T(8,128)S(1)} %constant_dynamic-slice_fusion), channel_id=1, source_target_pairs={{0,16},{2,18},{4,20},{6,22},{8,24},{10,26},{12,28},{14,30},{16,0},... | collective-permute-start | bytes 24584 | tf_op jit(solution)/shard_map/ppermute | solution.py:79
  8.8 0.1 collective-permute-start.1
  8.9 1.4 %fusion.11 = bf16[8,1,24,2048]{3,2,0,1:T(8,128)(2,1)S(1)} fusion(bf16[64,2048]{1,0:T(8,128)(2,1)} %param.12, f32[8,64]{1,0:T(8,128)S(1)} %get-tuple-element.9, f32[24]{0:T(128)S(1)} %iota_convert_fusion), kind=kOutput, calls=%fused_computation.14 | convolution fusion | flops 50737152 | bytes 1050720 | tf_op jit(solution)/shard_map/dot_general | solution.py:31
  10.3 0.2 collective-permute-done
  10.5 12.8 %collective-permute-done.1 = bf16[64,2048]{1,0:T(8,128)(2,1)S(1)} collective-permute-done((bf16[64,2048]{1,0:T(8,128)(2,1)}, bf16[64,2048]{1,0:T(8,128)(2,1)S(1)}, u32[]{:S(2)}, u32[]{:S(2)}) %collective-permute-start.1) | collective-permute-done | bytes 262176 | tf_op jit(solution)/shard_map/ppermute | solution.py:79
  23.3 0.4 fusion.12
  23.7 0.1 pad_maximum_fusion
  23.9 1.2 %copy.38 = bf16[8,2,24,2048]{3,2,1,0:T(8,128)(2,1)} copy(bf16[8,2,24,2048]{3,2,0,1:T(8,128)(2,1)S(1)} %pad_maximum_fusion) | data formatting | bytes 3145728 | tf_op jit(solution)/shard_map/concatenate | solution.py:101
  25.1 0.0 copy-start.1
  25.1 4.4 %all-to-all-start = ((bf16[8,2,24,2048]{3,2,1,0:T(8,128)(2,1)}), bf16[8,2,24,2048]{3,2,1,0:T(8,128)(2,1)}, u32[]{:S(2)}, u32[]{:S(2)}) async-start(bf16[8,2,24,2048]{3,2,1,0:T(8,128)(2,1)} %copy.38), calls=%async_computation | async-start | bytes 3145728 | tf_op jit(solution)/shard_map/all_to_all | solution.py:82
  29.5 0.0 copy-done.1
  29.5 1.2 collective-permute-start.3
  30.7 0.1 eq.188
  30.8 0.2 select_reduce_fusion.1
  31.0 0.1 mul.43
  31.1 0.1 mul.46
  31.1 0.1 bitcast_compare_fusion.1
  31.2 0.3 fusion.9
  31.6 20.0 %collective-permute-done.3 = bf16[64,2048]{1,0:T(8,128)(2,1)S(1)} collective-permute-done((bf16[64,2048]{1,0:T(8,128)(2,1)S(1)}, bf16[64,2048]{1,0:T(8,128)(2,1)S(1)}, u32[]{:S(2)}, u32[]{:S(2)}) %collective-permute-start.3) | collective-permute-done | bytes 262176 | tf_op jit(solution)/shard_map/ppermute | solution.py:79
  51.6 0.3 fusion.10
  51.9 1.3 %pad_maximum_fusion.1 = bf16[8,2,24,2048]{3,2,1,0:T(8,128)(2,1)} fusion(bf16[8,1,24,2048]{3,2,1,0:T(8,128)(2,1)S(1)} %bitcast.111, bf16[8,1,24,2048]{3,2,1,0:T(8,128)(2,1)S(1)} %bitcast.110), kind=kLoop, calls=%fused_computation.22 | loop fusion | flops 786432 | bytes 3145728 | tf_op jit(solution)/shard_map/concatenate | solution.py:101
  53.2 1.6 %all-to-all-done = bf16[8,2,24,2048]{3,2,1,0:T(8,128)(2,1)} async-done(((bf16[8,2,24,2048]{3,2,1,0:T(8,128)(2,1)}), bf16[8,2,24,2048]{3,2,1,0:T(8,128)(2,1)}, u32[]{:S(2)}, u32[]{:S(2)}) %all-to-all-start) | async-done | bytes 1572896 | tf_op jit(solution)/shard_map/all_to_all | solution.py:82
  54.8 7.2 %all-to-all-start.2 = ((bf16[8,2,24,2048]{3,2,1,0:T(8,128)(2,1)}), bf16[8,2,24,2048]{3,2,1,0:T(8,128)(2,1)}, u32[]{:S(2)}, u32[]{:S(2)}) async-start(bf16[8,2,24,2048]{3,2,1,0:T(8,128)(2,1)} %pad_maximum_fusion.1), calls=%async_computation.2 | async-start | bytes 3145728 | tf_op jit(solution)/shard_map/all_to_all | solution.py:82
  62.0 5.0 %fusion.4 = f32[384,704]{0,1:T(8,128)} fusion(bf16[384,2048]{1,0:T(8,128)(2,1)} %bitcast.14, bf16[1,2048,704]{1,2,0:T(8,128)(2,1)} %param.21), kind=kOutput, calls=%fused_computation.4 | convolution fusion | flops 1107296256 | bytes 5537792 | tf_op jit(solution)/shard_map/dot_general | solution.py:107
  67.0 0.0 copy-done
  67.0 6.7 %fusion.6 = bf16[384,2048]{1,0:T(8,128)(2,1)} fusion(bf16[1,704,2048]{2,1,0:T(8,128)(2,1)S(1)} %copy-done, bf16[384,2048]{1,0:T(8,128)(2,1)} %bitcast.14, bf16[1,2048,704]{1,2,0:T(8,128)(2,1)} %param.22, f32[384,704]{0,1:T(8,128)} %fusion.4), kind=kOutput, calls=%fused_computation.7 | convolution fusion | flops 2217000960 | bytes 9994240 | tf_op jit(solution)/shard_map/dot_general | solution.py:110
  73.7 8.0 %all-to-all-done.2 = bf16[8,2,24,2048]{3,2,1,0:T(8,128)(2,1)} async-done(((bf16[8,2,24,2048]{3,2,1,0:T(8,128)(2,1)}), bf16[8,2,24,2048]{3,2,1,0:T(8,128)(2,1)}, u32[]{:S(2)}, u32[]{:S(2)}) %all-to-all-start.2) | async-done | bytes 1572896 | tf_op jit(solution)/shard_map/all_to_all | solution.py:82
  81.8 4.3 %all-to-all-start.1 = ((bf16[8,2,24,2048]{3,2,1,0:T(8,128)(2,1)}), bf16[8,2,24,2048]{3,2,1,0:T(8,128)(2,1)}, u32[]{:S(2)}, u32[]{:S(2)}) async-start(bf16[8,2,24,2048]{3,2,1,0:T(8,128)(2,1)} %bitcast.113), calls=%async_computation.1 | async-start | bytes 3145728 | tf_op jit(solution)/shard_map/all_to_all | solution.py:82
  86.1 1.3 %copy.39 = bf16[1,384,704]{2,1,0:T(8,128)(2,1)S(1)} copy(bf16[1,384,704]{1,2,0:T(8,128)(2,1)} %param.20) | data formatting | bytes 1081344 | tf_op args[8]
  87.4 0.1 pad_maximum_fusion.2
  87.5 3.2 %convolution_convert_fusion.2 = bf16[704,1024]{1,0:T(8,128)(2,1)} fusion(bf16[384,704]{1,0:T(8,128)(2,1)S(1)} %bitcast.114, bf16[384,2048]{1,0:T(8,128)(2,1)} %bitcast.43, s32[]{:T(128)S(6)} %select_n.96), kind=kOutput, calls=%fused_computation.19 | convolution fusion | flops 554369024 | bytes 2768900 | tf_op jit(solution)/shard_map/dot_general | solution.py:134
  90.7 0.0 collective-permute-start.4
  90.7 0.8 fusion.28
  91.5 14.6 %all-to-all-done.1 = bf16[8,2,24,2048]{3,2,1,0:T(8,128)(2,1)} async-done(((bf16[8,2,24,2048]{3,2,1,0:T(8,128)(2,1)}), bf16[8,2,24,2048]{3,2,1,0:T(8,128)(2,1)}, u32[]{:S(2)}, u32[]{:S(2)}) %all-to-all-start.1) | async-done | bytes 1572896 | tf_op jit(solution)/shard_map/all_to_all | solution.py:82
  106.1 0.0 copy-start.4
  106.1 1.5 %fusion.46 = (bf16[8,1,24,2048]{3,2,1,0:T(8,128)(2,1)S(1)}, bf16[8,1,24,2048]{3,2,1,0:T(8,128)(2,1)S(1)}) fusion(bf16[8,2,24,2048]{3,2,1,0:T(8,128)(2,1)} %all-to-all-done.1), kind=kLoop, calls=%fused_computation.83 | loop fusion | bytes 3145728 | tf_op jit(solution)/shard_map/slice | solution.py:113
  107.7 0.0 copy-done.4
  107.7 0.3 fusion.48
  108.0 0.3 fusion.13
  108.3 0.0 copy-start.3
  108.3 0.0 copy-start.2
  108.3 0.1 collective-permute-start.2
  108.4 0.0 collective-permute-done.4
  108.4 4.1 %add_bitcast_fusion = f32[1,704,1024]{2,1,0:T(8,128)} fusion(bf16[704,1024]{1,0:T(8,128)(2,1)} %collective-permute-done.4, bf16[384,704]{1,0:T(8,128)(2,1)S(1)} %bitcast.115, bf16[384,2048]{1,0:T(8,128)(2,1)} %bitcast.43, s32[]{:T(128)S(6)} %select_n.95), kind=kOutput, calls=%fused_computation.6 | convolution fusion | flops 556531712 | bytes 5652484 | tf_op jit(solution)/shard_map/dot_general | solution.py:134
  112.5 0.0 copy-done.3
  112.5 0.3 fusion.47
  112.8 9.3 %collective-permute-done.2 = bf16[64,2048]{1,0:T(8,128)(2,1)S(1)} collective-permute-done((bf16[64,2048]{1,0:T(8,128)(2,1)S(1)}, bf16[64,2048]{1,0:T(8,128)(2,1)S(1)}, u32[]{:S(2)}, u32[]{:S(2)}) %collective-permute-start.2) | collective-permute-done | bytes 262176 | tf_op jit(solution)/shard_map/ppermute | solution.py:79
  122.1 0.0 copy-done.2
  122.1 1.0 add_convert_fusion
  (7 shorter events, 0.1 us)
Async XLA Ops:
  0.6 66.3 %copy-start = (bf16[1,704,2048]{2,1,0:T(8,128)(2,1)S(1)}, bf16[1,704,2048]{2,1,0:T(8,128)(2,1)}, u32[]{:S(2)}) copy-start(bf16[1,704,2048]{2,1,0:T(8,128)(2,1)} %param.23) | copy-start | bytes 8650756
  4.7 5.8 %collective-permute-start = (f32[4,64,8]{1,2,0:T(8,128)S(1)}, f32[4,64,8]{1,2,0:T(8,128)S(1)}, u32[]{:S(2)}, u32[]{:S(2)}) collective-permute-start(f32[4,64,8]{1,2,0:T(8,128)S(1)} %constant_dynamic-slice_fusion), channel_id=1, source_target_pairs={{0,16},{2,18},{4,20},{6,22},{8,24},{10,26},{12,28},{14,30},{16,0},... | collective-permute-start | bytes 24584 | tf_op jit(solution)/shard_map/ppermute | solution.py:79
  8.8 14.5 %collective-permute-start.1 = (bf16[64,2048]{1,0:T(8,128)(2,1)}, bf16[64,2048]{1,0:T(8,128)(2,1)S(1)}, u32[]{:S(2)}, u32[]{:S(2)}) collective-permute-start(bf16[64,2048]{1,0:T(8,128)(2,1)} %param.12), channel_id=1, source_target_pairs={{0,16},{2,18},{4,20},{6,22},{8,24},{10,26},{12,28},{14,30},{16,0},... | collective-permute-start | bytes 786440 | tf_op jit(solution)/shard_map/ppermute | solution.py:79
  25.1 4.4 %copy-start.1 = (bf16[64,2048]{1,0:T(8,128)(2,1)S(1)}, bf16[64,2048]{1,0:T(8,128)(2,1)}, u32[]{:S(2)}) copy-start(bf16[64,2048]{1,0:T(8,128)(2,1)} %param.16) | copy-start | bytes 786436
  25.1 29.7 %all-to-all-start = ((bf16[8,2,24,2048]{3,2,1,0:T(8,128)(2,1)}), bf16[8,2,24,2048]{3,2,1,0:T(8,128)(2,1)}, u32[]{:S(2)}, u32[]{:S(2)}) async-start(bf16[8,2,24,2048]{3,2,1,0:T(8,128)(2,1)} %copy.38), calls=%async_computation | async-start | bytes 3145728 | tf_op jit(solution)/shard_map/all_to_all | solution.py:82
  29.5 22.0 %collective-permute-start.3 = (bf16[64,2048]{1,0:T(8,128)(2,1)S(1)}, bf16[64,2048]{1,0:T(8,128)(2,1)S(1)}, u32[]{:S(2)}, u32[]{:S(2)}) collective-permute-start(bf16[64,2048]{1,0:T(8,128)(2,1)S(1)} %copy-done.1), channel_id=1, source_target_pairs={{0,16},{2,18},{4,20},{6,22},{8,24},{10,26},{12,28},{14,30},{16,0},... | collective-permute-start | bytes 786440 | tf_op jit(solution)/shard_map/ppermute | solution.py:79
  54.8 26.9 %all-to-all-start.2 = ((bf16[8,2,24,2048]{3,2,1,0:T(8,128)(2,1)}), bf16[8,2,24,2048]{3,2,1,0:T(8,128)(2,1)}, u32[]{:S(2)}, u32[]{:S(2)}) async-start(bf16[8,2,24,2048]{3,2,1,0:T(8,128)(2,1)} %pad_maximum_fusion.1), calls=%async_computation.2 | async-start | bytes 3145728 | tf_op jit(solution)/shard_map/all_to_all | solution.py:82
  81.8 24.4 %all-to-all-start.1 = ((bf16[8,2,24,2048]{3,2,1,0:T(8,128)(2,1)}), bf16[8,2,24,2048]{3,2,1,0:T(8,128)(2,1)}, u32[]{:S(2)}, u32[]{:S(2)}) async-start(bf16[8,2,24,2048]{3,2,1,0:T(8,128)(2,1)} %bitcast.113), calls=%async_computation.1 | async-start | bytes 3145728 | tf_op jit(solution)/shard_map/all_to_all | solution.py:82
  90.7 17.6 %collective-permute-start.4 = (bf16[704,1024]{1,0:T(8,128)(2,1)}, bf16[704,1024]{1,0:T(8,128)(2,1)}, u32[]{:S(2)}, u32[]{:S(2)}) collective-permute-start(bf16[704,1024]{1,0:T(8,128)(2,1)} %convolution_convert_fusion.2), channel_id=1, source_target_pairs={{0,1},{1,0},{2,3},{3,2},{4,5},{5,4},{6,7},{7,6},{8,9},{9,8},{10,11... | collective-permute-start | bytes 4325384 | tf_op jit(solution)/shard_map/ppermute | solution.py:137
  106.1 1.6 %copy-start.4 = (bf16[64,8,24]{0,2,1:T(8,128)(2,1)S(1)}, bf16[64,8,24]{0,2,1:T(8,128)(2,1)}, u32[]{:S(2)}) copy-start(bf16[64,8,24]{0,2,1:T(8,128)(2,1)} %get-tuple-element.19) | copy-start | bytes 73732
  108.3 4.2 %copy-start.3 = (bf16[64,8,24]{0,2,1:T(8,128)(2,1)S(1)}, bf16[64,8,24]{0,2,1:T(8,128)(2,1)}, u32[]{:S(2)}) copy-start(bf16[64,8,24]{0,2,1:T(8,128)(2,1)} %get-tuple-element.24) | copy-start | bytes 73732
  108.3 13.8 %copy-start.2 = (bf16[64,8,24]{0,2,1:T(8,128)(2,1)S(1)}, bf16[64,8,24]{0,2,1:T(8,128)(2,1)}, u32[]{:S(2)}) copy-start(bf16[64,8,24]{0,2,1:T(8,128)(2,1)} %get-tuple-element.25) | copy-start | bytes 73732
  108.3 13.8 %collective-permute-start.2 = (bf16[64,2048]{1,0:T(8,128)(2,1)S(1)}, bf16[64,2048]{1,0:T(8,128)(2,1)S(1)}, u32[]{:S(2)}, u32[]{:S(2)}) collective-permute-start(bf16[64,2048]{1,0:T(8,128)(2,1)S(1)} %fusion.13), channel_id=1, source_target_pairs={{0,16},{2,18},{4,20},{6,22},{8,24},{10,26},{12,28},{14,30},{16,0},... | collective-permute-start | bytes 786440 | tf_op jit(solution)/shard_map/ppermute | solution.py:79
